TPU v7x, 32 devices: a whole 2x2x4 slice. The times are simulated.
32 devices in a mesh: fsdp: 4 (over y, core), context: 4 (over z), tensor: 2 (over x).
Axes of the slice: x: 2, y: 2, z: 4, core: 2. Of those that a mesh axis runs over, the one named last changes fastest.
Arguments:
- hidden_in: float32 [4, 512, 2560], P('fsdp', 'context'), may hold values from -6 to 6
- cotangent: float32 [4, 512, 2560], P('fsdp', 'context'), may hold values from -6 to 6
- segment_ids: int32 [4, 512], P('fsdp', 'context'), may hold values from 0 to 3, as said below
- positions: int32 [4, 512], P('fsdp', 'context'), may hold values from 0 to 511, as said below
- attn_scale: float32 [2560], P(('fsdp', 'context')), may hold values from -0.5 to 0.5
- query_weight: float32 [2560, 2560], P(('fsdp', 'context'), 'tensor')
- keyval_weight: float32 [2560, 512], P(('fsdp', 'context'))
- output_weight: float32 [2560, 2560], P('tensor', ('fsdp', 'context')), may hold values from -0.5 to 0.5
- mlp_scale: float32 [2560], P(('fsdp', 'context')), may hold values from -0.5 to 0.5
- gate_weight: float32 [2560, 7680], P(('fsdp', 'context'), 'tensor'), may hold values from -0.125 to 0.125
- up_weight: float32 [2560, 7680], P(('fsdp', 'context'), 'tensor'), may hold values from -0.125 to 0.125
- down_weight: float32 [7680, 2560], P('tensor', ('fsdp', 'context')), may hold values from -0.0625 to 0.0625
- first_attn_scale: float32 [2560], P(('fsdp', 'context')), may hold values from -40 to 40
- first_query_weight: float32 [2560, 2560], P(('fsdp', 'context'), 'tensor'), may hold values from -16 to 16
- first_keyval_weight: float32 [2560, 512], P(('fsdp', 'context')), may hold values from -80 to 80
- first_output_weight: float32 [2560, 2560], P('tensor', ('fsdp', 'context')), may hold values from -4 to 4
- first_mlp_scale: float32 [2560], P(('fsdp', 'context')), may hold values from -20 to 20
- first_gate_weight: float32 [2560, 7680], P(('fsdp', 'context'), 'tensor'), may hold values from -16 to 16
- first_up_weight: float32 [2560, 7680], P(('fsdp', 'context'), 'tensor'), may hold values from -16 to 16
- first_down_weight: float32 [7680, 2560], P('tensor', ('fsdp', 'context')), may hold values from -24 to 24
- second_attn_scale: float32 [2560], P(('fsdp', 'context')), may hold values from 0.6144 to 6.144
- second_query_weight: float32 [2560, 2560], P(('fsdp', 'context'), 'tensor'), may hold values from 0.1024 to 1.024
- second_keyval_weight: float32 [2560, 512], P(('fsdp', 'context')), may hold values from 2.4576 to 24.576
- second_output_weight: float32 [2560, 2560], P('tensor', ('fsdp', 'context')), may hold values from 0.006 to 0.06
- second_mlp_scale: float32 [2560], P(('fsdp', 'context')), may hold values from 0.2048 to 2.048
- second_gate_weight: float32 [2560, 7680], P(('fsdp', 'context'), 'tensor'), may hold values from 0.1024 to 1.024
- second_up_weight: float32 [2560, 7680], P(('fsdp', 'context'), 'tensor'), may hold values from 0.1024 to 1.024
- second_down_weight: float32 [7680, 2560], P('tensor', ('fsdp', 'context')), may hold values from 0.2048 to 2.048
Outputs:
- block_output: float32 [4, 512, 2560], P('fsdp', 'context')
- input_grad: float32 [4, 512, 2560], P('fsdp', 'context')
- grad_attn_scale: float32 [2560], P(('fsdp', 'context'))
- grad_query_weight: float32 [2560, 2560], P(('fsdp', 'context'), 'tensor')
- grad_keyval_weight: float32 [2560, 512], P(('fsdp', 'context'))
- grad_output_weight: float32 [2560, 2560], P('tensor', ('fsdp', 'context'))
- grad_mlp_scale: float32 [2560], P(('fsdp', 'context'))
- grad_gate_weight: float32 [2560, 7680], P(('fsdp', 'context'), 'tensor')
- grad_up_weight: float32 [2560, 7680], P(('fsdp', 'context'), 'tensor')
- grad_down_weight: float32 [7680, 2560], P('tensor', ('fsdp', 'context'))
- new_attn_scale: float32 [2560], P(('fsdp', 'context'))
- new_query_weight: float32 [2560, 2560], P(('fsdp', 'context'), 'tensor')
- new_keyval_weight: float32 [2560, 512], P(('fsdp', 'context'))
- new_output_weight: float32 [2560, 2560], P('tensor', ('fsdp', 'context'))
- new_mlp_scale: float32 [2560], P(('fsdp', 'context'))
- new_gate_weight: float32 [2560, 7680], P(('fsdp', 'context'), 'tensor')
- new_up_weight: float32 [2560, 7680], P(('fsdp', 'context'), 'tensor')
- new_down_weight: float32 [7680, 2560], P('tensor', ('fsdp', 'context'))
- new_first_attn_scale: float32 [2560], P(('fsdp', 'context'))
- new_first_query_weight: float32 [2560, 2560], P(('fsdp', 'context'), 'tensor')
- new_first_keyval_weight: float32 [2560, 512], P(('fsdp', 'context'))
- new_first_output_weight: float32 [2560, 2560], P('tensor', ('fsdp', 'context'))
- new_first_mlp_scale: float32 [2560], P(('fsdp', 'context'))
- new_first_gate_weight: float32 [2560, 7680], P(('fsdp', 'context'), 'tensor')
- new_first_up_weight: float32 [2560, 7680], P(('fsdp', 'context'), 'tensor')
- new_first_down_weight: float32 [7680, 2560], P('tensor', ('fsdp', 'context'))
- new_second_attn_scale: float32 [2560], P(('fsdp', 'context'))
- new_second_query_weight: float32 [2560, 2560], P(('fsdp', 'context'), 'tensor')
- new_second_keyval_weight: float32 [2560, 512], P(('fsdp', 'context'))
- new_second_output_weight: float32 [2560, 2560], P('tensor', ('fsdp', 'context'))
- new_second_mlp_scale: float32 [2560], P(('fsdp', 'context'))
- new_second_gate_weight: float32 [2560, 7680], P(('fsdp', 'context'), 'tensor')
- new_second_up_weight: float32 [2560, 7680], P(('fsdp', 'context'), 'tensor')
- new_second_down_weight: float32 [7680, 2560], P('tensor', ('fsdp', 'context'))
Inputs may be any that keep to these rules, and one draw needn't show every extreme that they name: segment_ids start at 0 and never fall along a sequence; a document is a run of equal values; the first sequence is one document, every other sequence holds four. positions count the tokens from the first token of the token's document, which has 0.
All inputs are finite; a program needn't handle non-finite values.
Results may differ from a plain program's by a relative error of at most 0.014.
Values may be sent and summed in bfloat16 or wider, within the bound.
A program may use at most 448 MiB of HBM per device.

v0:
```python
import jax
import jax.numpy as jnp
from jax import lax
from jax.sharding import PartitionSpec as P

HD = 256
norm_eps = 1e-06
beta_one = 0.9
beta_two = 0.999
adam_eps = 1e-08
learn_rate = 0.03
decay_rate = 0.1
adam_step = 4.0
rope_base = 10000.0
masked_value = -1e30
single = jnp.float32
half_type = jnp.bfloat16


def gelu_tanh(values):
    return jax.nn.gelu(values, approximate=True)


def rope_tables(positions):
    half = HD // 2
    freq = rope_base ** (-2.0 * jnp.arange(half).astype(jnp.float32) / HD)
    angle = positions.astype(jnp.float32)[..., None] * freq
    return (jnp.cos(angle), jnp.sin(angle))


def rotate(values, cosine, sine):
    half = values.shape[-1] // 2
    first = values[..., :half]
    second = values[..., half:]
    return jnp.concatenate(
        [first * cosine - second * sine, second * cosine + first * sine], axis=-1
    )


def unrotate(values, cosine, sine):
    half = values.shape[-1] // 2
    first = values[..., :half]
    second = values[..., half:]
    return jnp.concatenate(
        [first * cosine + second * sine, second * cosine - first * sine], axis=-1
    )


def rms_forward(values, scale):
    inverse = lax.rsqrt(jnp.mean(values * values, axis=-1, keepdims=True) + norm_eps)
    normed = values * inverse
    return (normed, inverse, (normed * (1.0 + scale)).astype(jnp.bfloat16))


def rms_backward(dnorm, normed, inverse, scale):
    dnormed = dnorm * (1.0 + scale)
    dvalues = inverse * (dnormed - normed * jnp.mean(dnormed * normed, axis=-1, keepdims=True))
    return (dvalues, dnorm * normed)


def adamw(weight, grad, first, second):
    first_new = beta_one * first + (1.0 - beta_one) * grad
    second_new = beta_two * second + (1.0 - beta_two) * grad * grad
    fix_one = 1.0 - beta_one**adam_step
    fix_two = 1.0 - beta_two**adam_step
    update = first_new / fix_one / (jnp.sqrt(second_new / fix_two) + adam_eps)
    return (weight - learn_rate * (update + decay_rate * weight), first_new, second_new)


def dot(a, b, dims):
    return lax.dot_general(a, b, (dims, ((), ())), preferred_element_type=single)


def small_gather(attn_scale, mlp_scale, segment_ids):
    scales = jnp.stack([attn_scale, mlp_scale]).astype(half_type)
    scales = lax.all_gather(scales, ("fsdp", "context"), axis=1, tiled=True).astype(single)
    seg_all = lax.all_gather(segment_ids, "context", axis=1, tiled=True)
    return (scales[0], scales[1], seg_all)


def gather_rows(block):
    return lax.all_gather(block, ("fsdp", "context"), axis=0, tiled=True)


def prepare_slice(block):
    rows, columns = block.shape
    ctx = lax.axis_size("context")
    parts = block.reshape(rows, ctx, columns // ctx).transpose(1, 0, 2)
    parts = lax.all_to_all(parts, "context", split_axis=0, concat_axis=0, tiled=True)
    full = lax.all_gather(parts, "fsdp", axis=0, tiled=True)
    return full.reshape(-1, columns // ctx)


def gather_tokens(block):
    return lax.all_gather(block, ("context", "tensor"), axis=0, tiled=True)


def scatter_tokens(part):
    return lax.psum_scatter(
        part.astype(half_type), ("context", "tensor"), scatter_dimension=0, tiled=True
    ).astype(single)


def scatter_rows(part):
    return lax.psum_scatter(
        part.astype(half_type), ("fsdp", "context"), scatter_dimension=0, tiled=True
    ).astype(single)


def return_slice(part):
    full, columns = part.shape
    ctx = lax.axis_size("context")
    fs = lax.axis_size("fsdp")
    rows = full // (ctx * fs)
    parts = part.astype(half_type).reshape(fs * ctx, rows, columns)
    parts = lax.psum_scatter(parts, "fsdp", scatter_dimension=0, tiled=True)
    parts = lax.all_to_all(parts, "context", split_axis=0, concat_axis=0, tiled=True)
    return parts.transpose(1, 0, 2).reshape(rows, ctx * columns).astype(single)


def on_device(
    hidden_in,
    cotangent,
    segment_ids,
    positions,
    attn_scale,
    query_weight,
    keyval_weight,
    output_weight,
    mlp_scale,
    gate_weight,
    up_weight,
    down_weight,
    first_attn_scale,
    first_query_weight,
    first_keyval_weight,
    first_output_weight,
    first_mlp_scale,
    first_gate_weight,
    first_up_weight,
    first_down_weight,
    second_attn_scale,
    second_query_weight,
    second_keyval_weight,
    second_output_weight,
    second_mlp_scale,
    second_gate_weight,
    second_up_weight,
    second_down_weight,
):
    ten = lax.axis_size("tensor")
    x = lax.axis_index("tensor")
    context_index = lax.axis_index("context")
    block, width = hidden_in.shape[1:]
    half_rows = block // ten
    heads_here = query_weight.shape[1] // HD
    heads_width = heads_here * HD
    hidden = hidden_in[0]
    cot = cotangent[0]
    hidden_half = lax.dynamic_slice_in_dim(hidden, x * half_rows, half_rows, 0)
    cot_half = lax.dynamic_slice_in_dim(cot, x * half_rows, half_rows, 0)
    scale_one, scale_two, seg_all = small_gather(attn_scale, mlp_scale, segment_ids)
    query_full = gather_rows(query_weight.astype(half_type))
    keyval_full = gather_rows(keyval_weight.astype(half_type))
    output_full = gather_rows(output_weight.astype(half_type).T)
    gate_slice = prepare_slice(gate_weight.astype(half_type))
    up_slice = prepare_slice(up_weight.astype(half_type))
    down_slice = prepare_slice(down_weight.astype(half_type).T)
    dy_all = gather_tokens(cot_half.astype(half_type))
    normed_one, inv_one, low_one = rms_forward(hidden, scale_one)
    query = dot(low_one, query_full, ((1,), (0,))).reshape(block, heads_here, HD)
    keyval = dot(low_one, keyval_full, ((1,), (0,)))
    cosine, sine = rope_tables(positions[0])
    query_low = (rotate(query, cosine[:, None, :], sine[:, None, :]) * HD ** (-0.5)).astype(
        half_type
    )
    key_low = rotate(keyval[:, :HD], cosine, sine).astype(half_type)
    keyval_low = jnp.concatenate([key_low, keyval[:, HD:].astype(half_type)], axis=-1)
    keyval_all = lax.all_gather(keyval_low, "context", axis=0, tiled=True)
    keys_all = keyval_all[:, :HD]
    values_all = keyval_all[:, HD:]
    rows_index = context_index * block + jnp.arange(block, dtype=jnp.int32)
    cols_index = jnp.arange(keys_all.shape[0], dtype=jnp.int32)
    allowed = (rows_index[:, None] >= cols_index[None, :]) & (
        segment_ids[0][:, None] == seg_all[0][None, :]
    )
    scores = jnp.einsum("bhd,jd->hbj", query_low, keys_all, preferred_element_type=single)
    masked = jnp.where(allowed, scores, masked_value)
    top = jnp.max(masked, axis=-1, keepdims=True)
    total = jnp.sum(jnp.where(allowed, jnp.exp(masked - top), 0.0), axis=-1, keepdims=True)
    lse = top + jnp.log(total)
    prob = jnp.where(allowed, jnp.exp(masked - lse), 0.0)
    prob_low = prob.astype(half_type)
    att_low = jnp.einsum("hbj,jd->bhd", prob_low, values_all, preferred_element_type=single).astype(
        half_type
    )
    att_flat = att_low.reshape(block, heads_width)
    attn_part = dot(att_flat, output_full, ((1,), (1,)))
    attn_half = lax.psum_scatter(
        attn_part.astype(half_type), "tensor", scatter_dimension=0, tiled=True
    )
    mid_half = hidden_half + attn_half.astype(single)
    normed_two, inv_two, low_two = rms_forward(mid_half, scale_two)
    low_all = gather_tokens(low_two)
    gate = dot(low_all, gate_slice, ((1,), (0,)))
    upper = dot(low_all, up_slice, ((1,), (0,)))
    dhid = dot(dy_all, down_slice, ((1,), (0,)))
    gelu_gate, gelu_back = jax.vjp(gelu_tanh, gate)
    hid_low = (gelu_gate * upper).astype(half_type)
    dgate_low = gelu_back(dhid * upper)[0].astype(half_type)
    dup_low = (dhid * gelu_gate).astype(half_type)
    dnorm_two = scatter_tokens(
        dot(dgate_low, gate_slice, ((1,), (1,))) + dot(dup_low, up_slice, ((1,), (1,)))
    )
    mlp_half = scatter_tokens(dot(hid_low, down_slice, ((1,), (1,))))
    grad_wd = return_slice(dot(dy_all, hid_low, ((0,), (0,)))).T
    grad_wg = return_slice(dot(low_all, dgate_low, ((0,), (0,))))
    grad_wu = return_slice(dot(low_all, dup_low, ((0,), (0,))))
    dmid_norm, terms_two = rms_backward(dnorm_two, normed_two, inv_two, scale_two)
    dmid_half = cot_half + dmid_norm
    dmid_low = lax.all_gather(dmid_half.astype(half_type), "tensor", axis=0, tiled=True)
    grad_out_full = dot(dmid_low, att_flat, ((0,), (0,)))
    datt_low = (
        dot(dmid_low, output_full, ((1,), (0,))).astype(half_type).reshape(block, heads_here, HD)
    )
    delta = jnp.einsum("bhd,bhd->hb", datt_low, att_low, preferred_element_type=single)
    dprob = jnp.einsum("bhd,jd->hbj", datt_low, values_all, preferred_element_type=single)
    dscore_low = (prob * (dprob - delta[..., None])).astype(half_type)
    dquery = jnp.einsum("hbj,jd->bhd", dscore_low, keys_all, preferred_element_type=single)
    dkey_part = jnp.einsum("hbj,bhd->jd", dscore_low, query_low, preferred_element_type=single)
    dvalue_part = jnp.einsum("hbj,bhd->jd", prob_low, datt_low, preferred_element_type=single)
    dkeyval_own = lax.psum_scatter(
        jnp.concatenate([dkey_part, dvalue_part], axis=-1).astype(half_type),
        "context",
        scatter_dimension=0,
        tiled=True,
    )
    dkeyval_sum = lax.psum(dkeyval_own.astype(single), "tensor")
    dquery_low = (
        (unrotate(dquery, cosine[:, None, :], sine[:, None, :]) * HD ** (-0.5))
        .astype(half_type)
        .reshape(block, heads_width)
    )
    dnorm_query = dot(dquery_low, query_full, ((1,), (1,)))
    dnorm_query = lax.psum_scatter(
        dnorm_query.astype(half_type), "tensor", scatter_dimension=0, tiled=True
    ).astype(single)
    dkeyval_low = jnp.concatenate(
        [unrotate(dkeyval_sum[:, :HD], cosine, sine), dkeyval_sum[:, HD:]], axis=-1
    ).astype(half_type)
    dkeyval_half = lax.dynamic_slice_in_dim(dkeyval_low, x * half_rows, half_rows, 0)
    dnorm_one = dnorm_query + dot(dkeyval_half, keyval_full, ((1,), (1,)))
    normed_half = lax.dynamic_slice_in_dim(normed_one, x * half_rows, half_rows, 0)
    inv_half = lax.dynamic_slice_in_dim(inv_one, x * half_rows, half_rows, 0)
    dinput_norm, terms_one = rms_backward(dnorm_one, normed_half, inv_half, scale_one)
    grad_query_full = dot(low_one, dquery_low, ((0,), (0,)))
    grad_keyval_full = dot(low_one, dkeyval_low, ((0,), (0,)))
    grad_wq = scatter_rows(grad_query_full)
    grad_wkv = scatter_rows(grad_keyval_full)
    grad_wo = scatter_rows(grad_out_full).T
    terms = jnp.stack([jnp.sum(terms_one, axis=0), jnp.sum(terms_two, axis=0)])
    terms = lax.psum_scatter(terms, ("fsdp", "context"), scatter_dimension=1, tiled=True)
    terms = lax.psum(terms, "tensor")
    grad_s1, grad_s2 = (terms[0], terms[1])
    outs = jnp.stack([mid_half + mlp_half, dmid_half + dinput_norm])
    outs = lax.all_gather(outs, "tensor", axis=1, tiled=True)
    masters = (
        attn_scale,
        query_weight,
        keyval_weight,
        output_weight,
        mlp_scale,
        gate_weight,
        up_weight,
        down_weight,
    )
    grads = (grad_s1, grad_wq, grad_wkv, grad_wo, grad_s2, grad_wg, grad_wu, grad_wd)
    firsts = (
        first_attn_scale,
        first_query_weight,
        first_keyval_weight,
        first_output_weight,
        first_mlp_scale,
        first_gate_weight,
        first_up_weight,
        first_down_weight,
    )
    seconds = (
        second_attn_scale,
        second_query_weight,
        second_keyval_weight,
        second_output_weight,
        second_mlp_scale,
        second_gate_weight,
        second_up_weight,
        second_down_weight,
    )
    results = [
        adamw(weight, grad, first, second)
        for weight, grad, first, second in zip(masters, grads, firsts, seconds)
    ]
    return (
        outs[0][None],
        outs[1][None],
        *grads,
        *(entry[0] for entry in results),
        *(entry[1] for entry in results),
        *(entry[2] for entry in results),
    )


def solution(mesh):
    both = ("fsdp", "context")
    tokens = P("fsdp", "context", None)
    weights = (
        P(both),
        P(both, "tensor"),
        P(both, None),
        P("tensor", both),
        P(both),
        P(both, "tensor"),
        P(both, "tensor"),
        P("tensor", both),
    )
    return jax.shard_map(
        on_device,
        mesh=mesh,
        in_specs=(tokens, tokens, P("fsdp", "context"), P("fsdp", "context"), *weights * 3),
        out_specs=(tokens, tokens, *weights * 4),
        check_vma=False,
    )
```

profile of v0, /device:TPU:0, one launch (start us, length us, event | category | flops | bytes accessed | tf_op | source)
XLA Modules:
  0.0 1195.5 jit_solution(1834390715932010794)
XLA Ops:
  13.0 34.2 %all-gather = bf16[16,160,2]{1,2,0:T(2,128)(2,1)S(1)} all-gather(bf16[1,160,2]{1,2,0:T(2,128)(2,1)S(1)} %maximum_bitcast_fusion), channel_id=1, replica_groups=mesh['fsdp'=4,'context'=4,'tensor'=2] {'fsdp','context'}, dimensions={0}, use_global_device_ids=true | all-gather | bytes 10880 | tf_op jit(solution)/shard_map/all_gather | solution.py:76
  60.3 18.9 %all_gather.41 = bf16[512,512]{1,0:T(8,128)(2,1)S(1)} all-gather(bf16[128,512]{1,0:T(8,128)(2,1)S(1)} %pad_maximum_fusion.2), channel_id=1, replica_groups=mesh['fsdp'=4,'context'=4,'tensor'=2] {'context'}, dimensions={0}, use_global_device_ids=true | all-gather | bytes 655360 | tf_op jit(solution)/shard_map/all_gather | solution.py:179
  79.2 45.6 %all-gather.13.cloned.1.call-done = bf16[2560,1280]{1,0:T(8,128)(2,1)} async-done(((bf16[160,1280]{1,0:T(8,128)(2,1)}), bf16[2560,1280]{1,0:T(8,128)(2,1)}) %all-gather.13.cloned.1.call-update) | async-done | bytes 6553616 | tf_op jit(solution)/shard_map/all_gather | solution.py:82
  124.8 9.4 copy.192
  143.0 46.3 %all-gather.15.cloned.1.call-done = bf16[2560,1280]{1,0:T(8,128)(2,1)} async-done(((bf16[160,1280]{1,0:T(8,128)(2,1)}), bf16[2560,1280]{1,0:T(8,128)(2,1)}) %all-gather.15.cloned.1.call-update) | async-done | bytes 6553616 | tf_op jit(solution)/shard_map/all_gather | solution.py:82
  206.3 60.5 %all_to_all.30 = bf16[4,160,960]{2,1,0:T(8,128)(2,1)} all-to-all(bf16[4,160,960]{2,1,0:T(8,128)(2,1)S(1)} %copy.197), channel_id=1, replica_groups=mesh['fsdp'=4,'context'=4,'tensor'=2] {'context'}, dimensions={0} | all-to-all | bytes 2457600 | tf_op jit(solution)/shard_map/all_to_all | solution.py:89
  275.9 33.0 %all_to_all.31 = bf16[4,160,960]{2,1,0:T(8,128)(2,1)} all-to-all(bf16[4,160,960]{2,1,0:T(8,128)(2,1)S(1)} %copy.195), channel_id=1, replica_groups=mesh['fsdp'=4,'context'=4,'tensor'=2] {'context'}, dimensions={0} | all-to-all | bytes 2457600 | tf_op jit(solution)/shard_map/all_to_all | solution.py:89
  320.3 33.4 %all_to_all.32 = bf16[4,160,960]{2,1,0:T(8,128)(2,1)} all-to-all(bf16[4,160,960]{2,1,0:T(8,128)(2,1)S(1)} %copy.196), channel_id=1, replica_groups=mesh['fsdp'=4,'context'=4,'tensor'=2] {'context'}, dimensions={0} | all-to-all | bytes 2457600 | tf_op jit(solution)/shard_map/all_to_all | solution.py:89
  361.6 47.2 %all-gather.17.cloned.1.call-done = bf16[512,2560]{1,0:T(8,128)(2,1)} async-done(((bf16[64,2560]{1,0:T(8,128)(2,1)}), bf16[512,2560]{1,0:T(8,128)(2,1)}) %all-gather.17.cloned.1.call-update) | async-done | bytes 2621456 | tf_op jit(solution)/shard_map/all_gather | solution.py:95
  416.1 33.2 %all-gather.21.cloned.1.call-done = bf16[16,160,960]{2,1,0:T(8,128)(2,1)} async-done(((bf16[4,160,960]{2,1,0:T(8,128)(2,1)}), bf16[16,160,960]{2,1,0:T(8,128)(2,1)}) %all-gather.21.cloned.1.call-update) | async-done | bytes 4915216 | tf_op jit(solution)/shard_map/all_gather | solution.py:90
  449.3 9.6 multiply_convert_fusion.1
  473.9 63.9 %reduce-scatter.19.cloned.1.call-done = bf16[64,2560]{1,0:T(8,128)(2,1)} async-done(((bf16[512,2560]{1,0:T(8,128)(2,1)}), bf16[64,2560]{1,0:T(8,128)(2,1)}) %reduce-scatter.19.cloned.1.call-update) | async-done | bytes 327696 | tf_op jit(solution)/shard_map/reduce_scatter | solution.py:99
  539.1 72.4 %reduce-scatter.17.cloned.1.call-done = bf16[64,2560]{1,0:T(8,128)(2,1)} async-done(((bf16[512,2560]{1,0:T(8,128)(2,1)}), bf16[64,2560]{1,0:T(8,128)(2,1)}) %reduce-scatter.17.cloned.1.call-update) | async-done | bytes 327696 | tf_op jit(solution)/shard_map/reduce_scatter | solution.py:99
  613.8 8.7 all_gather.50
  667.8 7.9 copy.211
  676.4 13.2 %all-reduce.1 = f32[128,512]{1,0:T(8,128)S(1)} all-reduce(bf16[128,512]{1,0:T(8,128)(2,1)} %reduce-scatter.23.cloned.1.call-done), channel_id=1, replica_groups=mesh['fsdp'=4,'context'=4,'tensor'=2] {'tensor'}, use_global_device_ids=true, to_apply=%region_10.11 | all-reduce | flops 65536 | bytes 393216 | tf_op jit(solution)/shard_map/psum | solution.py:238
  703.6 7.8 copy.213
  737.2 44.2 %reduce-scatter.33.cloned.1.call-done = bf16[4,160,960]{2,1,0:T(8,128)(2,1)} async-done(((bf16[16,160,960]{2,1,0:T(8,128)(2,1)}), bf16[4,160,960]{2,1,0:T(8,128)(2,1)}) %reduce-scatter.33.cloned.1.call-update) | async-done | bytes 1228816 | tf_op jit(solution)/shard_map/reduce_scatter | solution.py:116
  786.0 58.0 %reduce-scatter.37.cloned.1.call-done = f32[160,2]{1,0:T(8,128)} async-done(((f32[2560,2]{1,0:T(8,128)}), f32[160,2]{1,0:T(8,128)}) %reduce-scatter.37.cloned.1.call-update) | async-done | bytes 1296
  849.9 47.0 %reduce-scatter.35.cloned.1.call-done = bf16[4,160,960]{2,1,0:T(8,128)(2,1)} async-done(((bf16[16,160,960]{2,1,0:T(8,128)(2,1)}), bf16[4,160,960]{2,1,0:T(8,128)(2,1)}) %reduce-scatter.35.cloned.1.call-update) | async-done | bytes 1228816 | tf_op jit(solution)/shard_map/reduce_scatter | solution.py:116
  902.6 35.4 %all-gather.27.cloned.1.call-done = f32[2,128,2560]{2,1,0:T(8,128)} async-done(((f32[2,64,2560]{2,1,0:T(8,128)}), f32[2,128,2560]{2,1,0:T(8,128)}) %all-gather.27.cloned.1.call-update) | async-done | bytes 2621456 | tf_op jit(solution)/shard_map/all_gather | solution.py:266
  941.4 64.5 %reduce-scatter.27.cloned.1.call-done = bf16[160,512]{1,0:T(8,128)(2,1)} async-done(((bf16[2560,512]{1,0:T(8,128)(2,1)}), bf16[160,512]{1,0:T(8,128)(2,1)}) %reduce-scatter.27.cloned.1.call-update) | async-done | bytes 163856 | tf_op jit(solution)/shard_map/reduce_scatter | solution.py:105
  1054.4 41.3 %reduce-scatter.25.cloned.1.call-done = bf16[160,1280]{1,0:T(8,128)(2,1)} async-done(((bf16[2560,1280]{1,0:T(8,128)(2,1)}), bf16[160,1280]{1,0:T(8,128)(2,1)}) %reduce-scatter.25.cloned.1.call-update) | async-done | bytes 409616 | tf_op jit(solution)/shard_map/reduce_scatter | solution.py:105
  1099.1 86.2 %reduce-scatter.29.cloned.1.call-done = bf16[160,1280]{1,0:T(8,128)(2,1)} async-done(((bf16[2560,1280]{1,0:T(8,128)(2,1)}), bf16[160,1280]{1,0:T(8,128)(2,1)}) %reduce-scatter.29.cloned.1.call-update) | async-done | bytes 409616 | tf_op jit(solution)/shard_map/reduce_scatter | solution.py:105
  (306 shorter events, 256.7 us)
Async XLA Ops:
  8.1 49.6 %all-gather.11.cloned.1.call-start = ((), (), s32[]{:S(2)}) async-start(), calls=%async_computation.18 | async-start | bytes 2785280 | tf_op jit(solution)/shard_map/all_gather | solution.py:82
  10.0 114.8 %all-gather.13.cloned.1.call-start = ((), (), s32[]{:S(2)}) async-start(), calls=%async_computation.19 | async-start | bytes 6963200 | tf_op jit(solution)/shard_map/all_gather | solution.py:82
  12.0 177.3 %all-gather.15.cloned.1.call-start = ((), (), s32[]{:S(2)}) async-start(), calls=%async_computation.20 | async-start | bytes 6963200 | tf_op jit(solution)/shard_map/all_gather | solution.py:82
  12.9 296.2 %reduce-scatter.15.cloned.1.call-start = ((), (), s32[]{:S(2)}) async-start(), calls=%async_computation.21 | async-start | bytes 983040 | tf_op jit(solution)/shard_map/reduce_scatter | solution.py:199
  195.3 159.0 %all-gather.25.cloned.1.call-start = ((), (), s32[]{:S(2)}) async-start(), calls=%async_computation.27 | async-start | bytes 2949120 | tf_op jit(solution)/shard_map/all_gather | solution.py:95
  197.2 157.1 %all-gather.23.cloned.1.call-start = ((), (), s32[]{:S(2)}) async-start(), calls=%async_computation.25 | async-start | bytes 6553600 | tf_op jit(solution)/shard_map/all_gather | solution.py:90
  266.9 94.7 %all-gather.19.cloned.1.call-start = ((), (), s32[]{:S(2)}) async-start(), calls=%async_computation.23 | async-start | bytes 6553600 | tf_op jit(solution)/shard_map/all_gather | solution.py:90
  309.0 99.9 %all-gather.17.cloned.1.call-start = ((), (), s32[]{:S(2)}) async-start(), calls=%async_computation.22 | async-start | bytes 2949120 | tf_op jit(solution)/shard_map/all_gather | solution.py:95
  311.1 138.2 %all-gather.21.cloned.1.call-start = ((), (), s32[]{:S(2)}) async-start(), calls=%async_computation.24 | async-start | bytes 6553600 | tf_op jit(solution)/shard_map/all_gather | solution.py:90
  353.7 184.0 %reduce-scatter.19.cloned.1.call-start = ((), (), s32[]{:S(2)}) async-start(), calls=%async_computation.28 | async-start | bytes 2949120 | tf_op jit(solution)/shard_map/reduce_scatter | solution.py:99
  466.5 144.9 %reduce-scatter.17.cloned.1.call-start = ((), (), s32[]{:S(2)}) async-start(), calls=%async_computation.26 | async-start | bytes 2949120 | tf_op jit(solution)/shard_map/reduce_scatter | solution.py:99
  473.8 202.6 %reduce-scatter.23.cloned.1.call-start = ((), (), s32[]{:S(2)}) async-start(), calls=%async_computation.30 | async-start | bytes 655360 | tf_op jit(solution)/shard_map/reduce_scatter | solution.py:232
  635.2 56.1 %reduce-scatter.21.cloned.1.call-start = ((), (), s32[]{:S(2)}) async-start(), calls=%async_computation.29 | async-start | bytes 983040 | tf_op jit(solution)/shard_map/reduce_scatter | solution.py:245
  645.7 81.8 %reduce-scatter.31.cloned.1.call-start = ((), (), s32[]{:S(2)}) async-start(), calls=%async_computation.35 | async-start | bytes 6553600 | tf_op jit(solution)/shard_map/reduce_scatter | solution.py:116
  660.6 120.8 %reduce-scatter.33.cloned.1.call-start = ((), (), s32[]{:S(2)}) async-start(), calls=%async_computation.36 | async-start | bytes 6553600 | tf_op jit(solution)/shard_map/reduce_scatter | solution.py:116
  675.7 168.3 %reduce-scatter.37.cloned.1.call-start = ((), (), s32[]{:S(2)}) async-start(), calls=%async_computation.38 | async-start | bytes 1392640
  696.6 200.4 %reduce-scatter.35.cloned.1.call-start = ((), (), s32[]{:S(2)}) async-start(), calls=%async_computation.37 | async-start | bytes 6553600 | tf_op jit(solution)/shard_map/reduce_scatter | solution.py:116
  711.5 226.5 %all-gather.27.cloned.1.call-start = ((), (), s32[]{:S(2)}) async-start(), calls=%async_computation.31 | async-start | bytes 3932160 | tf_op jit(solution)/shard_map/all_gather | solution.py:266
  715.3 290.7 %reduce-scatter.27.cloned.1.call-start = ((), (), s32[]{:S(2)}) async-start(), calls=%async_computation.33 | async-start | bytes 2785280 | tf_op jit(solution)/shard_map/reduce_scatter | solution.py:105
  717.8 377.9 %reduce-scatter.25.cloned.1.call-start = ((), (), s32[]{:S(2)}) async-start(), calls=%async_computation.32 | async-start | bytes 6963200 | tf_op jit(solution)/shard_map/reduce_scatter | solution.py:105
  727.5 53.9 %all-to-all-start.3 = ((bf16[4,160,960]{2,1,0:T(8,128)(2,1)}), bf16[4,160,960]{2,1,0:T(8,128)(2,1)S(1)}, u32[]{:S(2)}, u32[]{:S(2)}) async-start(bf16[4,160,960]{2,1,0:T(8,128)(2,1)} %reduce-scatter.31.cloned.1.call-done), calls=%async_computation.12 | async-start | bytes 2621440 | tf_op jit(solution)/shard_map/all_to_all | solution.py:117
  732.1 453.2 %reduce-scatter.29.cloned.1.call-start = ((), (), s32[]{:S(2)}) async-start(), calls=%async_computation.34 | async-start | bytes 6963200 | tf_op jit(solution)/shard_map/reduce_scatter | solution.py:105
  781.4 115.5 %all-to-all-start.4 = ((bf16[4,160,960]{2,1,0:T(8,128)(2,1)}), bf16[4,160,960]{2,1,0:T(8,128)(2,1)}, u32[]{:S(2)}, u32[]{:S(2)}) async-start(bf16[4,160,960]{2,1,0:T(8,128)(2,1)} %reduce-scatter.33.cloned.1.call-done), calls=%async_computation.14 | async-start | bytes 2621440 | tf_op jit(solution)/shard_map/all_to_all | solution.py:117
  896.9 128.2 %all-to-all-start.5 = ((bf16[4,160,960]{2,1,0:T(8,128)(2,1)}), bf16[4,160,960]{2,1,0:T(8,128)(2,1)}, u32[]{:S(2)}, u32[]{:S(2)}) async-start(bf16[4,160,960]{2,1,0:T(8,128)(2,1)} %reduce-scatter.35.cloned.1.call-done), calls=%async_computation.16 | async-start | bytes 2621440 | tf_op jit(solution)/shard_map/all_to_all | solution.py:117
  (74 other events, 2811.5 us)
Sparse Core Ops, SparseCore 0:
  11.8 45.8 all-gather.10
  60.5 64.2 all-gather.12
  127.7 61.5 all-gather.14
  195.4 15.1 reduce-scatter.14
  635.3 21.1 reduce-scatter.22
  659.2 14.3 reduce-scatter.20
  676.1 51.3 reduce-scatter.30
  730.0 51.3 reduce-scatter.32
  785.6 58.3 reduce-scatter.36
  846.4 50.4 reduce-scatter.34
  899.0 38.9 all-gather.26
  941.7 64.1 reduce-scatter.26
  1009.9 85.7 reduce-scatter.24
  1099.5 85.7 reduce-scatter.28
Sparse Core Ops, SparseCore 1:
  198.5 71.3 all-gather.24
  271.3 38.4 all-gather.22
  311.2 40.2 all-gather.18
  354.3 54.4 all-gather.16
  410.4 38.8 all-gather.20
  466.6 71.1 reduce-scatter.18
  541.1 70.3 reduce-scatter.16
where the time goes:
time: 1210 us; the launch traced here: 1200 us
  waiting for transfers between devices  692 us (57%)
  blocking collectives  214 us (18%)
  matrix products  106 us (9%)
  local copies, waits for them, and re-layouts  93.6 us (8%)
  other arithmetic  56.7 us (5%)
  between operations  16.8 us (1%)
  starting transfers between devices  15.7 us (1%)
    reduce_scatter x3, waiting for transfers between devices, scatter_rows(): lax.psum_scatter(part.astype(half_type), ('fsdp', 'context'), scatter_dim...  192 us
    reduce_scatter x2, waiting for transfers between devices, scatter_tokens(): lax.psum_scatter(part.astype(half_type), ('context', 'tensor'), scatter_d...  136 us
    all_to_all x3, blocking collectives, prepare_slice(): lax.all_to_all(parts, 'context', split_axis=0, concat_axis=0, tiled=True)  127 us
    dot_general x18, matrix products, dot(): lax.dot_general(a, b, (dims, ((), ())), preferred_element_type=single)  100 us
    reduce_scatter x3, waiting for transfers between devices, return_slice(): parts = lax.psum_scatter(parts, 'fsdp', scatter_dimension=0, tiled=True)  96.2 us
    all_gather x3, waiting for transfers between devices, gather_rows(): return lax.all_gather(block, ('fsdp', 'context'), axis=0, tiled=True)  93.5 us
    unnamed x22, waiting for transfers between devices  58.4 us
    all_gather x2, waiting for transfers between devices, gather_tokens(): return lax.all_gather(block, ('context', 'tensor'), axis=0, tiled=True)  47.3 us
  transfers between devices with their start and end apart: 24, of which 15 were waited for; matrix products, arithmetic and copies ran while one was open for 17% of the time, Pallas kernels for 0%

commit v1 on v0

--- a/solution.py
+++ b/solution.py
@@ -17,6 +17,18 @@
 half_type = jnp.bfloat16
 
 
+def doubled_up(value, axis, dim):
+    ways, here = (lax.axis_size(axis), lax.axis_index(axis))
+    grown, reach = (value, 1)
+    while reach < ways:
+        theirs = lax.ppermute(grown, axis, [(d, d ^ reach) for d in range(ways)])
+        mine_first = jnp.concatenate([grown, theirs], axis=dim)
+        theirs_first = jnp.concatenate([theirs, grown], axis=dim)
+        grown = jnp.where(here & reach == 0, mine_first, theirs_first)
+        reach = 2 * reach
+    return grown
+
+
 def gelu_tanh(values):
     return jax.nn.gelu(values, approximate=True)
 
@@ -79,7 +91,7 @@
 
 
 def gather_rows(block):
-    return lax.all_gather(block, ("fsdp", "context"), axis=0, tiled=True)
+    return doubled_up(block, ("fsdp", "context"), 0)
 
 
 def prepare_slice(block):

time: 1210 us -> 1340 us (1.11)
  waiting for transfers between devices: 692 us -> 794 us
  other arithmetic: 56.7 us -> 80.9 us
  starting transfers between devices: 15.7 us -> 30.5 us
    ppermute x0 -> x12, waiting for transfers between devices: none -> 193 us  [doubled_up(): theirs = lax.ppermute(grown, axis, [(d, d ^ reach) for d in range(ways)])]
    all_gather x3 -> x0, waiting for transfers between devices: 93.5 us -> none  [gather_rows(): return lax.all_gather(block, ('fsdp', 'context'), axis=0, tiled=True)]
    select_n x0 -> x9, other arithmetic: none -> 15.7 us  [doubled_up(): grown = jnp.where(here & reach == 0, mine_first, theirs_first)]
    ppermute x0 -> x12, starting transfers between devices: none -> 14.8 us  [doubled_up(): theirs = lax.ppermute(grown, axis, [(d, d ^ reach) for d in range(ways)])]
    unnamed x22 -> x19, waiting for transfers between devices: 58.4 us -> 58.3 us
  transfers between devices with their start and end apart: 24 -> 33, of which waited for: 15 -> 18; matrix products, arithmetic and copies ran while one was open for 17% -> 17% of each run, Pallas kernels for 0% -> 0%
where the time goes in v1:
time: 1340 us; the launch traced here: 1330 us
  waiting for transfers between devices  794 us (59%)
  blocking collectives  207 us (15%)
  matrix products  111 us (8%)
  local copies, waits for them, and re-layouts  93 us (7%)
  other arithmetic  80.9 us (6%)
  starting transfers between devices  30.5 us (2%)
  between operations  16.7 us (1%)
    reduce_scatter x3, waiting for transfers between devices, scatter_rows(): lax.psum_scatter(part.astype(half_type), ('fsdp', 'context'), scatter_dim...  193 us
    ppermute x12, waiting for transfers between devices, doubled_up(): theirs = lax.ppermute(grown, axis, [(d, d ^ reach) for d in range(ways)])  193 us
    reduce_scatter x2, waiting for transfers between devices, scatter_tokens(): lax.psum_scatter(part.astype(half_type), ('context', 'tensor'), scatter_d...  136 us
    all_to_all x3, blocking collectives, prepare_slice(): lax.all_to_all(parts, 'context', split_axis=0, concat_axis=0, tiled=True)  124 us
    dot_general x18, matrix products, dot(): lax.dot_general(a, b, (dims, ((), ())), preferred_element_type=single)  106 us
    reduce_scatter x3, waiting for transfers between devices, return_slice(): parts = lax.psum_scatter(parts, 'fsdp', scatter_dimension=0, tiled=True)  94.4 us
    unnamed x19, waiting for transfers between devices  58.3 us
    all_gather x2, waiting for transfers between devices, gather_tokens(): return lax.all_gather(block, ('context', 'tensor'), axis=0, tiled=True)  50.5 us
  transfers between devices with their start and end apart: 33, of which 18 were waited for; matrix products, arithmetic and copies ran while one was open for 17% of the time, Pallas kernels for 0%

profile of v1, /device:TPU:0, one launch (start us, length us, event | category | flops | bytes accessed | tf_op | source)
XLA Modules:
  0.0 1333.7 jit_solution(13122021714803440177)
XLA Ops:
  27.3 32.9 %collective-permute-done.5 = bf16[320,1280]{1,0:T(8,128)(2,1)} collective-permute-done((bf16[320,1280]{1,0:T(8,128)(2,1)S(1)}, bf16[320,1280]{1,0:T(8,128)(2,1)}, u32[]{:S(2)}, u32[]{:S(2)}) %collective-permute-start.5) | collective-permute-done | bytes 819232 | tf_op jit(solution)/shard_map/ppermute | solution.py:24
  62.7 32.9 %all-gather = bf16[16,160,2]{1,2,0:T(2,128)(2,1)S(1)} all-gather(bf16[1,160,2]{1,2,0:T(2,128)(2,1)S(1)} %maximum_bitcast_fusion), channel_id=1, replica_groups=mesh['fsdp'=4,'context'=4,'tensor'=2] {'fsdp','context'}, dimensions={0}, use_global_device_ids=true | all-gather | bytes 10880 | tf_op jit(solution)/shard_map/all_gather | solution.py:88
  113.0 25.6 %collective-permute-done.1 = bf16[320,512]{1,0:T(8,128)(2,1)S(1)} collective-permute-done((bf16[320,512]{1,0:T(8,128)(2,1)S(1)}, bf16[320,512]{1,0:T(8,128)(2,1)S(1)}, u32[]{:S(2)}, u32[]{:S(2)}) %collective-permute-start.1) | collective-permute-done | bytes 327712 | tf_op jit(solution)/shard_map/ppermute | solution.py:24
  146.0 10.0 collective-permute-done.9
  158.6 85.5 %collective-permute-done.3 = bf16[1280,512]{1,0:T(8,128)(2,1)} collective-permute-done((bf16[1280,512]{1,0:T(8,128)(2,1)}, bf16[1280,512]{1,0:T(8,128)(2,1)}, u32[]{:S(2)}, u32[]{:S(2)}) %collective-permute-start.3) | collective-permute-done | bytes 1310752 | tf_op jit(solution)/shard_map/ppermute | solution.py:24
  251.2 15.5 %all_gather.31 = bf16[512,512]{1,0:T(8,128)(2,1)S(1)} all-gather(bf16[128,512]{1,0:T(8,128)(2,1)S(1)} %pad_maximum_fusion.2), channel_id=1, replica_groups=mesh['fsdp'=4,'context'=4,'tensor'=2] {'context'}, dimensions={0}, use_global_device_ids=true | all-gather | bytes 655360 | tf_op jit(solution)/shard_map/all_gather | solution.py:191
  266.7 9.6 fusion.17
  293.1 29.5 %collective-permute-done.11 = bf16[1280,1280]{1,0:T(8,128)(2,1)} collective-permute-done((bf16[1280,1280]{1,0:T(8,128)(2,1)}, bf16[1280,1280]{1,0:T(8,128)(2,1)}, u32[]{:S(2)}, u32[]{:S(2)}) %collective-permute-start.11) | collective-permute-done | bytes 3276832 | tf_op jit(solution)/shard_map/ppermute | solution.py:24
  341.2 60.0 %all_to_all.30 = bf16[4,160,960]{2,1,0:T(8,128)(2,1)} all-to-all(bf16[4,160,960]{2,1,0:T(8,128)(2,1)S(1)} %copy.238), channel_id=1, replica_groups=mesh['fsdp'=4,'context'=4,'tensor'=2] {'context'}, dimensions={0} | all-to-all | bytes 2457600 | tf_op jit(solution)/shard_map/all_to_all | solution.py:101
  410.2 31.4 %all_to_all.31 = bf16[4,160,960]{2,1,0:T(8,128)(2,1)} all-to-all(bf16[4,160,960]{2,1,0:T(8,128)(2,1)S(1)} %copy.236), channel_id=1, replica_groups=mesh['fsdp'=4,'context'=4,'tensor'=2] {'context'}, dimensions={0} | all-to-all | bytes 2457600 | tf_op jit(solution)/shard_map/all_to_all | solution.py:101
  452.8 32.8 %all_to_all.32 = bf16[4,160,960]{2,1,0:T(8,128)(2,1)} all-to-all(bf16[4,160,960]{2,1,0:T(8,128)(2,1)S(1)} %copy.237), channel_id=1, replica_groups=mesh['fsdp'=4,'context'=4,'tensor'=2] {'context'}, dimensions={0} | all-to-all | bytes 2457600 | tf_op jit(solution)/shard_map/all_to_all | solution.py:101
  493.3 50.5 %all-gather.8.cloned.1.call-done = bf16[512,2560]{1,0:T(8,128)(2,1)} async-done(((bf16[64,2560]{1,0:T(8,128)(2,1)}), bf16[512,2560]{1,0:T(8,128)(2,1)}) %all-gather.8.cloned.1.call-update) | async-done | bytes 2621456 | tf_op jit(solution)/shard_map/all_gather | solution.py:107
  551.1 33.2 %all-gather.12.cloned.1.call-done = bf16[16,160,960]{2,1,0:T(8,128)(2,1)} async-done(((bf16[4,160,960]{2,1,0:T(8,128)(2,1)}), bf16[16,160,960]{2,1,0:T(8,128)(2,1)}) %all-gather.12.cloned.1.call-update) | async-done | bytes 4915216 | tf_op jit(solution)/shard_map/all_gather | solution.py:102
  584.3 9.6 multiply_convert_fusion.1
  608.8 63.9 %reduce-scatter.19.cloned.1.call-done = bf16[64,2560]{1,0:T(8,128)(2,1)} async-done(((bf16[512,2560]{1,0:T(8,128)(2,1)}), bf16[64,2560]{1,0:T(8,128)(2,1)}) %reduce-scatter.19.cloned.1.call-update) | async-done | bytes 327696 | tf_op jit(solution)/shard_map/reduce_scatter | solution.py:111
  674.0 72.0 %reduce-scatter.17.cloned.1.call-done = bf16[64,2560]{1,0:T(8,128)(2,1)} async-done(((bf16[512,2560]{1,0:T(8,128)(2,1)}), bf16[64,2560]{1,0:T(8,128)(2,1)}) %reduce-scatter.17.cloned.1.call-update) | async-done | bytes 327696 | tf_op jit(solution)/shard_map/reduce_scatter | solution.py:111
  814.5 13.4 %all-reduce.1 = f32[128,512]{1,0:T(8,128)S(1)} all-reduce(bf16[128,512]{1,0:T(8,128)(2,1)} %reduce-scatter.23.cloned.1.call-done), channel_id=1, replica_groups=mesh['fsdp'=4,'context'=4,'tensor'=2] {'tensor'}, use_global_device_ids=true, to_apply=%region_10.11 | all-reduce | flops 65536 | bytes 393216 | tf_op jit(solution)/shard_map/psum | solution.py:250
  874.8 44.1 %reduce-scatter.33.cloned.1.call-done = bf16[4,160,960]{2,1,0:T(8,128)(2,1)} async-done(((bf16[16,160,960]{2,1,0:T(8,128)(2,1)}), bf16[4,160,960]{2,1,0:T(8,128)(2,1)}) %reduce-scatter.33.cloned.1.call-update) | async-done | bytes 1228816 | tf_op jit(solution)/shard_map/reduce_scatter | solution.py:128
  923.5 58.0 %reduce-scatter.37.cloned.1.call-done = f32[160,2]{1,0:T(8,128)} async-done(((f32[2560,2]{1,0:T(8,128)}), f32[160,2]{1,0:T(8,128)}) %reduce-scatter.37.cloned.1.call-update) | async-done | bytes 1296
  987.4 47.1 %reduce-scatter.35.cloned.1.call-done = bf16[4,160,960]{2,1,0:T(8,128)(2,1)} async-done(((bf16[16,160,960]{2,1,0:T(8,128)(2,1)}), bf16[4,160,960]{2,1,0:T(8,128)(2,1)}) %reduce-scatter.35.cloned.1.call-update) | async-done | bytes 1228816 | tf_op jit(solution)/shard_map/reduce_scatter | solution.py:128
  1039.9 35.7 %all-gather.18.cloned.1.call-done = f32[2,128,2560]{2,1,0:T(8,128)} async-done(((f32[2,64,2560]{2,1,0:T(8,128)}), f32[2,128,2560]{2,1,0:T(8,128)}) %all-gather.18.cloned.1.call-update) | async-done | bytes 2621456 | tf_op jit(solution)/shard_map/all_gather | solution.py:278
  1079.0 64.6 %reduce-scatter.27.cloned.1.call-done = bf16[160,512]{1,0:T(8,128)(2,1)} async-done(((bf16[2560,512]{1,0:T(8,128)(2,1)}), bf16[160,512]{1,0:T(8,128)(2,1)}) %reduce-scatter.27.cloned.1.call-update) | async-done | bytes 163856 | tf_op jit(solution)/shard_map/reduce_scatter | solution.py:117
  1191.2 42.0 %reduce-scatter.25.cloned.1.call-done = bf16[160,1280]{1,0:T(8,128)(2,1)} async-done(((bf16[2560,1280]{1,0:T(8,128)(2,1)}), bf16[160,1280]{1,0:T(8,128)(2,1)}) %reduce-scatter.25.cloned.1.call-update) | async-done | bytes 409616 | tf_op jit(solution)/shard_map/reduce_scatter | solution.py:117
  1236.4 86.6 %reduce-scatter.29.cloned.1.call-done = bf16[160,1280]{1,0:T(8,128)(2,1)} async-done(((bf16[2560,1280]{1,0:T(8,128)(2,1)}), bf16[160,1280]{1,0:T(8,128)(2,1)}) %reduce-scatter.29.cloned.1.call-update) | async-done | bytes 409616 | tf_op jit(solution)/shard_map/reduce_scatter | solution.py:117
  (311 shorter events, 330.7 us)
Async XLA Ops:
  8.1 433.6 %reduce-scatter.15.cloned.1.call-start = ((), (), s32[]{:S(2)}) async-start(), calls=%async_computation.18 | async-start | bytes 983040 | tf_op jit(solution)/shard_map/reduce_scatter | solution.py:211
  25.1 80.7 %collective-permute-start = (bf16[160,512]{1,0:T(8,128)(2,1)S(1)}, bf16[160,512]{1,0:T(8,128)(2,1)}, u32[]{:S(2)}, u32[]{:S(2)}) collective-permute-start(bf16[160,512]{1,0:T(8,128)(2,1)S(1)} %convert_element_type.181), channel_id=1, source_target_pairs={{0,2},{2,0},{4,6},{6,4},{8,10},{10,8},{12,14},{14,12},{16,18},{18,... | collective-permute-start | bytes 491528 | tf_op jit(solution)/shard_map/ppermute | solution.py:24
  26.8 81.3 %collective-permute-start.8 = (bf16[160,1280]{1,0:T(8,128)(2,1)S(1)}, bf16[160,1280]{1,0:T(8,128)(2,1)}, u32[]{:S(2)}, u32[]{:S(2)}) collective-permute-start(bf16[160,1280]{1,0:T(8,128)(2,1)S(1)} %convert_bitcast_fusion.5), channel_id=1, source_target_pairs={{0,2},{2,0},{4,6},{6,4},{8,10},{10,8},{12,14},{14,12},{16,18},{18,... | collective-permute-start | bytes 1228808 | tf_op jit(solution)/shard_map/ppermute | solution.py:24
  142.4 124.3 %collective-permute-start.7 = (bf16[1280,1280]{1,0:T(8,128)(2,1)}, bf16[1280,1280]{1,0:T(8,128)(2,1)}, u32[]{:S(2)}, u32[]{:S(2)}) collective-permute-start(bf16[1280,1280]{1,0:T(8,128)(2,1)} %maximum_select_fusion.2), channel_id=1, source_target_pairs={{0,16},{2,18},{4,20},{6,22},{8,24},{10,26},{12,28},{14,30},{16,0},... | collective-permute-start | bytes 9830408 | tf_op jit(solution)/shard_map/ppermute | solution.py:24
  145.4 98.7 %collective-permute-start.3 = (bf16[1280,512]{1,0:T(8,128)(2,1)}, bf16[1280,512]{1,0:T(8,128)(2,1)}, u32[]{:S(2)}, u32[]{:S(2)}) collective-permute-start(bf16[1280,512]{1,0:T(8,128)(2,1)} %maximum_select_fusion.7), channel_id=1, source_target_pairs={{0,16},{2,18},{4,20},{6,22},{8,24},{10,26},{12,28},{14,30},{16,0},... | collective-permute-start | bytes 3932168 | tf_op jit(solution)/shard_map/ppermute | solution.py:24
  158.4 89.3 %collective-permute-start.10 = (bf16[640,1280]{1,0:T(8,128)(2,1)S(1)}, bf16[640,1280]{1,0:T(8,128)(2,1)S(1)}, u32[]{:S(2)}, u32[]{:S(2)}) collective-permute-start(bf16[640,1280]{1,0:T(8,128)(2,1)S(1)} %maximum_select_fusion.6), channel_id=1, source_target_pairs={{0,8},{2,10},{4,12},{6,14},{8,0},{10,2},{12,4},{14,6},{16,24},{18,... | collective-permute-start | bytes 4915208 | tf_op jit(solution)/shard_map/ppermute | solution.py:24
  329.8 156.2 %all-gather.16.cloned.1.call-start = ((), (), s32[]{:S(2)}) async-start(), calls=%async_computation.24 | async-start | bytes 2949120 | tf_op jit(solution)/shard_map/all_gather | solution.py:107
  331.7 154.3 %all-gather.14.cloned.1.call-start = ((), (), s32[]{:S(2)}) async-start(), calls=%async_computation.22 | async-start | bytes 6553600 | tf_op jit(solution)/shard_map/all_gather | solution.py:102
  401.2 92.1 %all-gather.10.cloned.1.call-start = ((), (), s32[]{:S(2)}) async-start(), calls=%async_computation.20 | async-start | bytes 6553600 | tf_op jit(solution)/shard_map/all_gather | solution.py:102
  441.6 102.2 %all-gather.8.cloned.1.call-start = ((), (), s32[]{:S(2)}) async-start(), calls=%async_computation.19 | async-start | bytes 2949120 | tf_op jit(solution)/shard_map/all_gather | solution.py:107
  443.7 140.5 %all-gather.12.cloned.1.call-start = ((), (), s32[]{:S(2)}) async-start(), calls=%async_computation.21 | async-start | bytes 6553600 | tf_op jit(solution)/shard_map/all_gather | solution.py:102
  485.7 187.0 %reduce-scatter.19.cloned.1.call-start = ((), (), s32[]{:S(2)}) async-start(), calls=%async_computation.25 | async-start | bytes 2949120 | tf_op jit(solution)/shard_map/reduce_scatter | solution.py:111
  601.5 144.5 %reduce-scatter.17.cloned.1.call-start = ((), (), s32[]{:S(2)}) async-start(), calls=%async_computation.23 | async-start | bytes 2949120 | tf_op jit(solution)/shard_map/reduce_scatter | solution.py:111
  608.8 205.8 %reduce-scatter.23.cloned.1.call-start = ((), (), s32[]{:S(2)}) async-start(), calls=%async_computation.27 | async-start | bytes 655360 | tf_op jit(solution)/shard_map/reduce_scatter | solution.py:244
  783.6 81.5 %reduce-scatter.31.cloned.1.call-start = ((), (), s32[]{:S(2)}) async-start(), calls=%async_computation.32 | async-start | bytes 6553600 | tf_op jit(solution)/shard_map/reduce_scatter | solution.py:128
  798.5 120.4 %reduce-scatter.33.cloned.1.call-start = ((), (), s32[]{:S(2)}) async-start(), calls=%async_computation.33 | async-start | bytes 6553600 | tf_op jit(solution)/shard_map/reduce_scatter | solution.py:128
  813.9 167.6 %reduce-scatter.37.cloned.1.call-start = ((), (), s32[]{:S(2)}) async-start(), calls=%async_computation.35 | async-start | bytes 1392640
  835.9 198.5 %reduce-scatter.35.cloned.1.call-start = ((), (), s32[]{:S(2)}) async-start(), calls=%async_computation.34 | async-start | bytes 6553600 | tf_op jit(solution)/shard_map/reduce_scatter | solution.py:128
  850.9 224.7 %all-gather.18.cloned.1.call-start = ((), (), s32[]{:S(2)}) async-start(), calls=%async_computation.28 | async-start | bytes 3932160 | tf_op jit(solution)/shard_map/all_gather | solution.py:278
  854.6 289.0 %reduce-scatter.27.cloned.1.call-start = ((), (), s32[]{:S(2)}) async-start(), calls=%async_computation.30 | async-start | bytes 2785280 | tf_op jit(solution)/shard_map/reduce_scatter | solution.py:117
  857.2 376.1 %reduce-scatter.25.cloned.1.call-start = ((), (), s32[]{:S(2)}) async-start(), calls=%async_computation.29 | async-start | bytes 6963200 | tf_op jit(solution)/shard_map/reduce_scatter | solution.py:117
  869.8 453.2 %reduce-scatter.29.cloned.1.call-start = ((), (), s32[]{:S(2)}) async-start(), calls=%async_computation.31 | async-start | bytes 6963200 | tf_op jit(solution)/shard_map/reduce_scatter | solution.py:117
  918.9 115.5 %all-to-all-start.4 = ((bf16[4,160,960]{2,1,0:T(8,128)(2,1)}), bf16[4,160,960]{2,1,0:T(8,128)(2,1)S(1)}, u32[]{:S(2)}, u32[]{:S(2)}) async-start(bf16[4,160,960]{2,1,0:T(8,128)(2,1)} %reduce-scatter.33.cloned.1.call-done), calls=%async_computation.14 | async-start | bytes 2621440 | tf_op jit(solution)/shard_map/all_to_all | solution.py:129
  1034.5 126.9 %all-to-all-start.5 = ((bf16[4,160,960]{2,1,0:T(8,128)(2,1)}), bf16[4,160,960]{2,1,0:T(8,128)(2,1)}, u32[]{:S(2)}, u32[]{:S(2)}) async-start(bf16[4,160,960]{2,1,0:T(8,128)(2,1)} %reduce-scatter.35.cloned.1.call-done), calls=%async_computation.16 | async-start | bytes 2621440 | tf_op jit(solution)/shard_map/all_to_all | solution.py:129
  (73 other events, 3464.0 us)
Sparse Core Ops, SparseCore 0:
  329.9 15.6 reduce-scatter.14
  772.7 21.3 reduce-scatter.22
  797.0 14.3 reduce-scatter.20
  813.8 51.3 reduce-scatter.30
  867.5 51.3 reduce-scatter.32
  923.0 58.4 reduce-scatter.36
  984.0 50.3 reduce-scatter.34
  1036.6 38.9 all-gather.17
  1079.4 64.2 reduce-scatter.26
  1147.4 85.7 reduce-scatter.24
  1237.2 85.7 reduce-scatter.28
Sparse Core Ops, SparseCore 1:
  333.0 71.1 all-gather.15
  405.6 39.2 all-gather.13
  446.2 40.2 all-gather.9
  489.3 54.4 all-gather.7
  545.4 38.8 all-gather.11
  601.6 71.1 reduce-scatter.18
  676.1 69.8 reduce-scatter.16
